TPU v7x, 256 devices: a whole 4x4x8 slice. The times are simulated.
256 devices in a mesh: section: 8 (over x, core), expert: 32 (over z, y).
Axes of the slice: x: 4, y: 4, z: 8, core: 2. Of those that a mesh axis runs over, the one named last changes fastest.
Arguments:
- tokens: bfloat16 [4, 1024, 2048], P(None, 'expert'), may hold values from -6 to 6
- attn_norm: float32 [8, 2048], P('section'), may hold values from 0.5 to 2
- moe_norm: float32 [8, 2048], P('section'), may hold values from 0.5 to 2
- query_weight: bfloat16 [8, 2048, 1024], P('section', 'expert'), may hold values from -4 to 4
- key_weight: bfloat16 [8, 2048, 128], P('section', 'expert'), may hold values from -0.125 to 0.125
- value_weight: bfloat16 [8, 2048, 128], P('section', 'expert'), may hold values from -0.125 to 0.125
- out_weight: bfloat16 [8, 1024, 2048], P('section', 'expert'), may hold values from -0.1875 to 0.1875
- gate_proj: bfloat16 [8, 32, 2048, 704], P('section', 'expert'), may hold values from -0.125 to 0.125
- up_proj: bfloat16 [8, 32, 2048, 704], P('section', 'expert'), may hold values from -0.125 to 0.125
- down_proj: bfloat16 [8, 32, 704, 2048], P('section', 'expert'), may hold values from -0.21875 to 0.21875
- routes: int32 [8, 4, 1024, 6], P('section', None, 'expert'), may hold values from 0 to 31, all different within a row; in each aligned block of 32 rows (0 to 31, 32 to 63, ..., all dimensions but the last counted through in order) at most 8 rows name the same one
- weights_code: int32 [8, 4, 1024, 6], P('section', None, 'expert'), may hold values from 8 to 64
Outputs:
- hidden_states: bfloat16 [8, 4, 1024, 2048], P('section', None, 'expert')
Inputs may be any that keep to these rules, and one draw needn't show every extreme that they name: `routes`: each row names 6 different experts. In each aligned block of 32 rows (one sequence's tokens of one micro-batch of one layer) no expert is named by more than 8 rows, a bound that some block reaches.
All inputs are finite; a program needn't handle non-finite values.
Results may differ from a plain program's by a relative error of at most 0.03.
Values may be sent and summed in bfloat16 or wider, within the bound.
No kernel may reach another device: no remote copies, remote signals or barrier semaphores. Data moves between devices by JAX's collectives and lax.ppermute only.
A program may use at most 128 MiB of HBM per device.

v0:
```python
import jax
import jax.numpy as jnp
from jax import lax
from jax.sharding import PartitionSpec as P

epsilon = 1e-06


def shifted(value, axis, steps):
    count = lax.axis_size(axis)
    initial, last = (max(0, -steps), min(count, count - steps))
    return lax.ppermute(value, axis, [(source, source + steps) for source in range(initial, last)])


def rms_scale(features, gain_vector):
    return (
        features
        * lax.rsqrt(jnp.mean(features * features, axis=-1, keepdims=True) + epsilon)
        * gain_vector
    )


def expert_rows(slot_rows, gate_matrix, up_matrix, down_matrix):
    gated = jnp.dot(slot_rows, gate_matrix, preferred_element_type=jnp.float32)
    lifted = jnp.dot(slot_rows, up_matrix, preferred_element_type=jnp.float32)
    hidden = (jax.nn.silu(gated) * lifted).astype(jnp.bfloat16)
    return jnp.dot(hidden, down_matrix, preferred_element_type=jnp.float32).astype(jnp.bfloat16)


def route_tables(picks_block, codes_block, expert_count, capacity):
    tok_rows, pick_count = picks_block.shape
    flat_ids = picks_block.reshape(-1)
    matches = (flat_ids[:, None] == jnp.arange(expert_count, dtype=jnp.int32)[None, :]).astype(
        jnp.int32
    )
    slot_ranks = jnp.sum((jnp.cumsum(matches, axis=0) - matches) * matches, axis=1)
    columns = flat_ids * capacity + slot_ranks
    onehot = (
        columns[:, None] == jnp.arange(expert_count * capacity, dtype=jnp.int32)[None, :]
    ).astype(jnp.float32)
    onehot = onehot.reshape(tok_rows, pick_count, expert_count * capacity)
    scatter_table = jnp.sum(onehot, axis=1).astype(jnp.bfloat16)
    pick_weights = codes_block.astype(jnp.float32) / 64.0
    combine_table = jnp.sum(onehot * pick_weights[:, :, None], axis=1).astype(jnp.bfloat16)
    return (scatter_table, combine_table)


def shards(
    tokens,
    attn_norm,
    moe_norm,
    query_weight,
    key_weight,
    value_weight,
    out_weight,
    gate_proj,
    up_proj,
    down_proj,
    routes,
    weights_code,
):
    section_count = lax.axis_size("section")
    section_index = lax.axis_index("section")
    expert_devices = lax.axis_size("expert")
    micro_count, tok_rows, model_width = tokens.shape
    pick_count = routes.shape[3]
    expert_count = expert_devices * gate_proj.shape[1]
    capacity = min(tok_rows, tok_rows * pick_count * 4 // (3 * expert_count))
    full_query, full_key, full_value, full_out = (
        lax.all_gather(query_weight, "expert", axis=1, tiled=True),
        lax.all_gather(key_weight, "expert", axis=1, tiled=True),
        lax.all_gather(value_weight, "expert", axis=1, tiled=True),
        lax.all_gather(out_weight, "expert", axis=1, tiled=True),
    )
    full_query = full_query[0]
    full_key = full_key[0]
    full_value = full_value[0]
    full_out = full_out[0]
    head_size = full_key.shape[-1]
    head_count = full_query.shape[-1] // head_size
    length = micro_count * tok_rows
    score_scale = head_size ** (-0.5)
    attn_gain = attn_norm[0]
    moe_gain = moe_norm[0]
    gate_matrix = gate_proj[0, 0]
    up_matrix = up_proj[0, 0]
    down_matrix = down_proj[0, 0]
    route_layer = routes[0]
    code_layer = weights_code[0]

    def feed_rows(slot_rows):
        return expert_rows(slot_rows, gate_matrix, up_matrix, down_matrix)

    def blank_rows(slot_rows):
        return jnp.zeros((slot_rows.shape[0], model_width), jnp.bfloat16)

    def advance(tick_index, state_carry):
        inbound, key_cache, value_cache, stored = state_carry
        block_index = tick_index - section_index
        active = (block_index >= 0) & (block_index < micro_count)
        clipped = jnp.clip(block_index, 0, micro_count - 1)
        first_rows = lax.dynamic_index_in_dim(tokens, clipped, 0, keepdims=False)
        layer_input = jnp.where(section_index == 0, first_rows, inbound)
        picks_block = lax.dynamic_index_in_dim(route_layer, clipped, 0, keepdims=False)
        codes_block = lax.dynamic_index_in_dim(code_layer, clipped, 0, keepdims=False)
        scatter_table, combine_table = route_tables(
            picks_block, codes_block, expert_count, capacity
        )
        wide_input = layer_input.astype(jnp.float32)
        moe_input = rms_scale(wide_input, moe_gain).astype(jnp.bfloat16)

        def attend(caches):
            old_keys, old_values = caches
            normed = rms_scale(wide_input, attn_gain).astype(jnp.bfloat16)
            query_rows = jnp.dot(normed, full_query, preferred_element_type=jnp.float32).astype(
                jnp.bfloat16
            )
            query_rows = query_rows.reshape(tok_rows, head_count, head_size)
            new_keys = jnp.dot(normed, full_key, preferred_element_type=jnp.float32).astype(
                jnp.bfloat16
            )
            new_values = jnp.dot(normed, full_value, preferred_element_type=jnp.float32).astype(
                jnp.bfloat16
            )
            offset = clipped * tok_rows
            key_vectors = lax.dynamic_update_slice_in_dim(old_keys, new_keys, offset, 0)
            value_vectors = lax.dynamic_update_slice_in_dim(old_values, new_values, offset, 0)
            attention_scores = (
                jnp.einsum(
                    "qhd,kd->hqk", query_rows, key_vectors, preferred_element_type=jnp.float32
                )
                * score_scale
            )
            positions = offset + jnp.arange(tok_rows, dtype=jnp.int32)
            causal = jnp.arange(length, dtype=jnp.int32)[None, :] <= positions[:, None]
            attention_scores = jnp.where(causal[None], attention_scores, -1e30)
            highest = jnp.max(attention_scores, axis=-1, keepdims=True)
            exponent = jnp.exp(attention_scores - highest)
            attention_probabilities = (exponent / jnp.sum(exponent, axis=-1, keepdims=True)).astype(
                jnp.bfloat16
            )
            attended_values = jnp.einsum(
                "hqk,kd->qhd",
                attention_probabilities,
                value_vectors,
                preferred_element_type=jnp.float32,
            )
            attended_values = attended_values.astype(jnp.bfloat16).reshape(
                tok_rows, head_count * head_size
            )
            attended = jnp.dot(attended_values, full_out, preferred_element_type=jnp.float32)
            return (attended, key_vectors, value_vectors)

        def skipped(caches):
            return (jnp.zeros((tok_rows, model_width), jnp.float32), caches[0], caches[1])

        attended, key_cache, value_cache = lax.cond(
            active, attend, skipped, (key_cache, value_cache)
        )
        outgoing = jnp.einsum(
            "te,td->ed", scatter_table, moe_input, preferred_element_type=jnp.float32
        )
        outgoing = outgoing.astype(jnp.bfloat16).reshape(expert_count, capacity, model_width)
        arrived = lax.all_to_all(outgoing, "expert", split_axis=0, concat_axis=0, tiled=True)
        slot_rows = arrived.reshape(-1, model_width)
        produced = lax.cond(active, feed_rows, blank_rows, slot_rows).reshape(arrived.shape)
        returned = lax.all_to_all(produced, "expert", split_axis=0, concat_axis=0, tiled=True)
        mixed = jnp.dot(
            combine_table, returned.reshape(-1, model_width), preferred_element_type=jnp.float32
        )
        output_rows = (wide_input + attended + mixed).astype(jnp.bfloat16)
        updated = lax.dynamic_update_index_in_dim(stored, output_rows, clipped, 0)
        stored = jnp.where(active, updated, stored)
        inbound = shifted(output_rows, "section", 1)
        return (inbound, key_cache, value_cache, stored)

    initial = (
        jnp.zeros((tok_rows, model_width), jnp.bfloat16),
        jnp.zeros((length, head_size), jnp.bfloat16),
        jnp.zeros((length, head_size), jnp.bfloat16),
        jnp.zeros((micro_count, tok_rows, model_width), jnp.bfloat16),
    )
    finals = lax.fori_loop(0, micro_count + section_count - 1, advance, initial)
    return finals[3][None]


def solution(mesh):
    placed = (
        P(None, "expert", None),
        P("section", None),
        P("section", None),
        P("section", "expert", None),
        P("section", "expert", None),
        P("section", "expert", None),
        P("section", "expert", None),
        P("section", "expert", None, None),
        P("section", "expert", None, None),
        P("section", "expert", None, None),
        P("section", None, "expert", None),
        P("section", None, "expert", None),
    )
    return jax.shard_map(
        shards,
        mesh=mesh,
        in_specs=placed,
        out_specs=P("section", None, "expert", None),
        check_vma=False,
    )
```

profile of v0, /device:TPU:10, one launch (start us, length us, event | category | flops | bytes accessed | tf_op | source)
XLA Modules:
  0.0 1040.3 jit_solution(5070451524895726768)
XLA Ops:
  17.4 52.8 %all_gather.13 = bf16[1,2048,128]{2,1,0:T(8,128)(2,1)S(1)} all-gather(bf16[1,64,128]{2,1,0:T(8,128)(2,1)S(1)} %copy-done.3), channel_id=1, replica_groups=mesh['section'=8,'expert'=32] {'expert'}, dimensions={1}, use_global_device_ids=true | all-gather | bytes 540672 | tf_op jit(solution)/shard_map/all_gather | solution.py:71
  70.1 47.8 %all_gather.12 = bf16[1,2048,128]{2,1,0:T(8,128)(2,1)S(1)} all-gather(bf16[1,64,128]{2,1,0:T(8,128)(2,1)S(1)} %copy-done.4), channel_id=1, replica_groups=mesh['section'=8,'expert'=32] {'expert'}, dimensions={1}, use_global_device_ids=true | all-gather | bytes 540672 | tf_op jit(solution)/shard_map/all_gather | solution.py:72
  118.0 57.3 %all-gather.5.cloned.1.call-done = bf16[1,1024,2048]{2,1,0:T(8,128)(2,1)} async-done(((bf16[1,32,2048]{2,1,0:T(8,128)(2,1)}), bf16[1,1024,2048]{2,1,0:T(8,128)(2,1)}) %all-gather.5.cloned.1.call-update) | async-done | bytes 4194320 | tf_op jit(solution)/shard_map/all_gather | solution.py:73
  175.4 857.3 %while.20 = (s32[]{:T(128)}, bf16[32,2048]{1,0:T(8,128)(2,1)S(1)}, bf16[128,128]{1,0:T(8,128)(2,1)S(1)}, bf16[128,128]{1,0:T(8,128)(2,1)S(1)}, bf16[4,32,2048]{2...) while((s32[]{:T(128)}, bf16[32,2048]{1,0:T(8,128)(2,1)S(1)}, ...), condition=%wide.region_14.15_spmd, body=%wide.region_0.14_spmd.sunk | while | flops 2613929216 | bytes 35623652 | solution.py:183
  186.4 25.4 %all-to-all-done = bf16[32,8,2048]{2,1,0:T(8,128)(2,1)S(1)} async-done(((bf16[32,8,2048]{2,1,0:T(8,128)(2,1)}), bf16[32,8,2048]{2,1,0:T(8,128)(2,1)S(1)}, u32[]{:S(2)}, u32[]{:S(2)}) %all-to-all-start) | async-done | bytes 1048608 | tf_op jit(solution)/shard_map/while/body/eval_jaxpr/all_to_all | solution.py:164
  218.6 25.2 %all-to-all-done.1 = bf16[32,8,2048]{2,1,0:T(8,128)(2,1)S(1)} async-done(((bf16[32,8,2048]{2,1,0:T(8,128)(2,1)}), bf16[32,8,2048]{2,1,0:T(8,128)(2,1)S(1)}, u32[]{:S(2)}, u32[]{:S(2)}) %all-to-all-start.1) | async-done | bytes 1048608 | tf_op jit(solution)/shard_map/while/body/eval_jaxpr/all_to_all | solution.py:167
  260.0 27.3 %all-to-all-done = bf16[32,8,2048]{2,1,0:T(8,128)(2,1)S(1)} async-done(((bf16[32,8,2048]{2,1,0:T(8,128)(2,1)}), bf16[32,8,2048]{2,1,0:T(8,128)(2,1)S(1)}, u32[]{:S(2)}, u32[]{:S(2)}) %all-to-all-start) | async-done | bytes 1048608 | tf_op jit(solution)/shard_map/while/body/eval_jaxpr/all_to_all | solution.py:164
  294.1 26.7 %all-to-all-done.1 = bf16[32,8,2048]{2,1,0:T(8,128)(2,1)S(1)} async-done(((bf16[32,8,2048]{2,1,0:T(8,128)(2,1)}), bf16[32,8,2048]{2,1,0:T(8,128)(2,1)S(1)}, u32[]{:S(2)}, u32[]{:S(2)}) %all-to-all-start.1) | async-done | bytes 1048608 | tf_op jit(solution)/shard_map/while/body/eval_jaxpr/all_to_all | solution.py:167
  345.0 19.0 %all-to-all-done = bf16[32,8,2048]{2,1,0:T(8,128)(2,1)S(1)} async-done(((bf16[32,8,2048]{2,1,0:T(8,128)(2,1)}), bf16[32,8,2048]{2,1,0:T(8,128)(2,1)S(1)}, u32[]{:S(2)}, u32[]{:S(2)}) %all-to-all-start) | async-done | bytes 1048608 | tf_op jit(solution)/shard_map/while/body/eval_jaxpr/all_to_all | solution.py:164
  401.4 17.6 %collective-permute-done = bf16[32,2048]{1,0:T(8,128)(2,1)S(1)} collective-permute-done((bf16[32,2048]{1,0:T(8,128)(2,1)S(1)}, bf16[32,2048]{1,0:T(8,128)(2,1)S(1)}, u32[]{:S(2)}, u32[]{:S(2)}) %collective-permute-start) | collective-permute-done | bytes 131104 | tf_op jit(solution)/shard_map/while/body/eval_jaxpr/ppermute | solution.py:12
  429.8 18.2 %all-to-all-done = bf16[32,8,2048]{2,1,0:T(8,128)(2,1)S(1)} async-done(((bf16[32,8,2048]{2,1,0:T(8,128)(2,1)}), bf16[32,8,2048]{2,1,0:T(8,128)(2,1)S(1)}, u32[]{:S(2)}, u32[]{:S(2)}) %all-to-all-start) | async-done | bytes 1048608 | tf_op jit(solution)/shard_map/while/body/eval_jaxpr/all_to_all | solution.py:164
  485.5 18.4 %collective-permute-done = bf16[32,2048]{1,0:T(8,128)(2,1)S(1)} collective-permute-done((bf16[32,2048]{1,0:T(8,128)(2,1)S(1)}, bf16[32,2048]{1,0:T(8,128)(2,1)S(1)}, u32[]{:S(2)}, u32[]{:S(2)}) %collective-permute-start) | collective-permute-done | bytes 131104 | tf_op jit(solution)/shard_map/while/body/eval_jaxpr/ppermute | solution.py:12
  514.7 18.2 %all-to-all-done = bf16[32,8,2048]{2,1,0:T(8,128)(2,1)S(1)} async-done(((bf16[32,8,2048]{2,1,0:T(8,128)(2,1)}), bf16[32,8,2048]{2,1,0:T(8,128)(2,1)S(1)}, u32[]{:S(2)}, u32[]{:S(2)}) %all-to-all-start) | async-done | bytes 1048608 | tf_op jit(solution)/shard_map/while/body/eval_jaxpr/all_to_all | solution.py:164
  593.0 18.2 %all-to-all-done = bf16[32,8,2048]{2,1,0:T(8,128)(2,1)S(1)} async-done(((bf16[32,8,2048]{2,1,0:T(8,128)(2,1)}), bf16[32,8,2048]{2,1,0:T(8,128)(2,1)S(1)}, u32[]{:S(2)}, u32[]{:S(2)}) %all-to-all-start) | async-done | bytes 1048608 | tf_op jit(solution)/shard_map/while/body/eval_jaxpr/all_to_all | solution.py:164
  667.9 19.5 %all-to-all-done = bf16[32,8,2048]{2,1,0:T(8,128)(2,1)S(1)} async-done(((bf16[32,8,2048]{2,1,0:T(8,128)(2,1)}), bf16[32,8,2048]{2,1,0:T(8,128)(2,1)S(1)}, u32[]{:S(2)}, u32[]{:S(2)}) %all-to-all-start) | async-done | bytes 1048608 | tf_op jit(solution)/shard_map/while/body/eval_jaxpr/all_to_all | solution.py:164
  694.5 28.7 %all-to-all-done.1 = bf16[32,8,2048]{2,1,0:T(8,128)(2,1)S(1)} async-done(((bf16[32,8,2048]{2,1,0:T(8,128)(2,1)}), bf16[32,8,2048]{2,1,0:T(8,128)(2,1)S(1)}, u32[]{:S(2)}, u32[]{:S(2)}) %all-to-all-start.1) | async-done | bytes 1048608 | tf_op jit(solution)/shard_map/while/body/eval_jaxpr/all_to_all | solution.py:167
  742.4 23.4 %all-to-all-done = bf16[32,8,2048]{2,1,0:T(8,128)(2,1)S(1)} async-done(((bf16[32,8,2048]{2,1,0:T(8,128)(2,1)}), bf16[32,8,2048]{2,1,0:T(8,128)(2,1)S(1)}, u32[]{:S(2)}, u32[]{:S(2)}) %all-to-all-start) | async-done | bytes 1048608 | tf_op jit(solution)/shard_map/while/body/eval_jaxpr/all_to_all | solution.py:164
  772.5 23.7 %all-to-all-done.1 = bf16[32,8,2048]{2,1,0:T(8,128)(2,1)S(1)} async-done(((bf16[32,8,2048]{2,1,0:T(8,128)(2,1)}), bf16[32,8,2048]{2,1,0:T(8,128)(2,1)S(1)}, u32[]{:S(2)}, u32[]{:S(2)}) %all-to-all-start.1) | async-done | bytes 1048608 | tf_op jit(solution)/shard_map/while/body/eval_jaxpr/all_to_all | solution.py:167
  816.9 22.2 %all-to-all-done = bf16[32,8,2048]{2,1,0:T(8,128)(2,1)S(1)} async-done(((bf16[32,8,2048]{2,1,0:T(8,128)(2,1)}), bf16[32,8,2048]{2,1,0:T(8,128)(2,1)S(1)}, u32[]{:S(2)}, u32[]{:S(2)}) %all-to-all-start) | async-done | bytes 1048608 | tf_op jit(solution)/shard_map/while/body/eval_jaxpr/all_to_all | solution.py:164
  845.8 22.3 %all-to-all-done.1 = bf16[32,8,2048]{2,1,0:T(8,128)(2,1)S(1)} async-done(((bf16[32,8,2048]{2,1,0:T(8,128)(2,1)}), bf16[32,8,2048]{2,1,0:T(8,128)(2,1)S(1)}, u32[]{:S(2)}, u32[]{:S(2)}) %all-to-all-start.1) | async-done | bytes 1048608 | tf_op jit(solution)/shard_map/while/body/eval_jaxpr/all_to_all | solution.py:167
  891.5 21.1 %all-to-all-done = bf16[32,8,2048]{2,1,0:T(8,128)(2,1)S(1)} async-done(((bf16[32,8,2048]{2,1,0:T(8,128)(2,1)}), bf16[32,8,2048]{2,1,0:T(8,128)(2,1)S(1)}, u32[]{:S(2)}, u32[]{:S(2)}) %all-to-all-start) | async-done | bytes 1048608 | tf_op jit(solution)/shard_map/while/body/eval_jaxpr/all_to_all | solution.py:164
  919.3 20.8 %all-to-all-done.1 = bf16[32,8,2048]{2,1,0:T(8,128)(2,1)S(1)} async-done(((bf16[32,8,2048]{2,1,0:T(8,128)(2,1)}), bf16[32,8,2048]{2,1,0:T(8,128)(2,1)S(1)}, u32[]{:S(2)}, u32[]{:S(2)}) %all-to-all-start.1) | async-done | bytes 1048608 | tf_op jit(solution)/shard_map/while/body/eval_jaxpr/all_to_all | solution.py:167
  966.0 26.8 %all-to-all-done = bf16[32,8,2048]{2,1,0:T(8,128)(2,1)S(1)} async-done(((bf16[32,8,2048]{2,1,0:T(8,128)(2,1)}), bf16[32,8,2048]{2,1,0:T(8,128)(2,1)S(1)}, u32[]{:S(2)}, u32[]{:S(2)}) %all-to-all-start) | async-done | bytes 1048608 | tf_op jit(solution)/shard_map/while/body/eval_jaxpr/all_to_all | solution.py:164
  999.6 26.4 %all-to-all-done.1 = bf16[32,8,2048]{2,1,0:T(8,128)(2,1)S(1)} async-done(((bf16[32,8,2048]{2,1,0:T(8,128)(2,1)}), bf16[32,8,2048]{2,1,0:T(8,128)(2,1)S(1)}, u32[]{:S(2)}, u32[]{:S(2)}) %all-to-all-start.1) | async-done | bytes 1048608 | tf_op jit(solution)/shard_map/while/body/eval_jaxpr/all_to_all | solution.py:167
  (395 shorter events, 503.0 us)
Async XLA Ops:
  6.5 111.5 %all-gather.3.cloned.1.call-start = ((), (), s32[]{:S(2)}) async-start(), calls=%async_computation.2 | async-start | bytes 4325376 | tf_op jit(solution)/shard_map/all_gather | solution.py:70
  7.3 168.0 %all-gather.5.cloned.1.call-start = ((), (), s32[]{:S(2)}) async-start(), calls=%async_computation.3 | async-start | bytes 4325376 | tf_op jit(solution)/shard_map/all_gather | solution.py:73
  179.5 32.4 %all-to-all-start = ((bf16[32,8,2048]{2,1,0:T(8,128)(2,1)}), bf16[32,8,2048]{2,1,0:T(8,128)(2,1)S(1)}, u32[]{:S(2)}, u32[]{:S(2)}) async-start(bf16[32,8,2048]{2,1,0:T(8,128)(2,1)} %fusion.71), calls=%async_computation | async-start | bytes 2097152 | tf_op jit(solution)/shard_map/while/body/eval_jaxpr/all_to_all | solution.py:164
  213.0 30.8 %all-to-all-start.1 = ((bf16[32,8,2048]{2,1,0:T(8,128)(2,1)}), bf16[32,8,2048]{2,1,0:T(8,128)(2,1)S(1)}, u32[]{:S(2)}, u32[]{:S(2)}) async-start(bf16[32,8,2048]{2,1,0:T(8,128)(2,1)} %bitcast.125), calls=%async_computation.1 | async-start | bytes 2097152 | tf_op jit(solution)/shard_map/while/body/eval_jaxpr/all_to_all | solution.py:167
  254.4 32.9 %all-to-all-start = ((bf16[32,8,2048]{2,1,0:T(8,128)(2,1)}), bf16[32,8,2048]{2,1,0:T(8,128)(2,1)S(1)}, u32[]{:S(2)}, u32[]{:S(2)}) async-start(bf16[32,8,2048]{2,1,0:T(8,128)(2,1)} %fusion.71), calls=%async_computation | async-start | bytes 2097152 | tf_op jit(solution)/shard_map/while/body/eval_jaxpr/all_to_all | solution.py:164
  288.5 32.4 %all-to-all-start.1 = ((bf16[32,8,2048]{2,1,0:T(8,128)(2,1)}), bf16[32,8,2048]{2,1,0:T(8,128)(2,1)S(1)}, u32[]{:S(2)}, u32[]{:S(2)}) async-start(bf16[32,8,2048]{2,1,0:T(8,128)(2,1)} %bitcast.125), calls=%async_computation.1 | async-start | bytes 2097152 | tf_op jit(solution)/shard_map/while/body/eval_jaxpr/all_to_all | solution.py:167
  338.3 25.7 %all-to-all-start = ((bf16[32,8,2048]{2,1,0:T(8,128)(2,1)}), bf16[32,8,2048]{2,1,0:T(8,128)(2,1)S(1)}, u32[]{:S(2)}, u32[]{:S(2)}) async-start(bf16[32,8,2048]{2,1,0:T(8,128)(2,1)} %fusion.71), calls=%async_computation | async-start | bytes 2097152 | tf_op jit(solution)/shard_map/while/body/eval_jaxpr/all_to_all | solution.py:164
  375.4 23.8 %all-to-all-start.1 = ((bf16[32,8,2048]{2,1,0:T(8,128)(2,1)}), bf16[32,8,2048]{2,1,0:T(8,128)(2,1)S(1)}, u32[]{:S(2)}, u32[]{:S(2)}) async-start(bf16[32,8,2048]{2,1,0:T(8,128)(2,1)} %bitcast.125), calls=%async_computation.1 | async-start | bytes 2097152 | tf_op jit(solution)/shard_map/while/body/eval_jaxpr/all_to_all | solution.py:167
  423.1 24.9 %all-to-all-start = ((bf16[32,8,2048]{2,1,0:T(8,128)(2,1)}), bf16[32,8,2048]{2,1,0:T(8,128)(2,1)S(1)}, u32[]{:S(2)}, u32[]{:S(2)}) async-start(bf16[32,8,2048]{2,1,0:T(8,128)(2,1)} %fusion.71), calls=%async_computation | async-start | bytes 2097152 | tf_op jit(solution)/shard_map/while/body/eval_jaxpr/all_to_all | solution.py:164
  459.5 23.8 %all-to-all-start.1 = ((bf16[32,8,2048]{2,1,0:T(8,128)(2,1)}), bf16[32,8,2048]{2,1,0:T(8,128)(2,1)S(1)}, u32[]{:S(2)}, u32[]{:S(2)}) async-start(bf16[32,8,2048]{2,1,0:T(8,128)(2,1)} %bitcast.125), calls=%async_computation.1 | async-start | bytes 2097152 | tf_op jit(solution)/shard_map/while/body/eval_jaxpr/all_to_all | solution.py:167
  508.0 24.9 %all-to-all-start = ((bf16[32,8,2048]{2,1,0:T(8,128)(2,1)}), bf16[32,8,2048]{2,1,0:T(8,128)(2,1)S(1)}, u32[]{:S(2)}, u32[]{:S(2)}) async-start(bf16[32,8,2048]{2,1,0:T(8,128)(2,1)} %fusion.71), calls=%async_computation | async-start | bytes 2097152 | tf_op jit(solution)/shard_map/while/body/eval_jaxpr/all_to_all | solution.py:164
  544.3 23.8 %all-to-all-start.1 = ((bf16[32,8,2048]{2,1,0:T(8,128)(2,1)}), bf16[32,8,2048]{2,1,0:T(8,128)(2,1)S(1)}, u32[]{:S(2)}, u32[]{:S(2)}) async-start(bf16[32,8,2048]{2,1,0:T(8,128)(2,1)} %bitcast.125), calls=%async_computation.1 | async-start | bytes 2097152 | tf_op jit(solution)/shard_map/while/body/eval_jaxpr/all_to_all | solution.py:167
  587.4 23.8 %all-to-all-start = ((bf16[32,8,2048]{2,1,0:T(8,128)(2,1)}), bf16[32,8,2048]{2,1,0:T(8,128)(2,1)S(1)}, u32[]{:S(2)}, u32[]{:S(2)}) async-start(bf16[32,8,2048]{2,1,0:T(8,128)(2,1)} %fusion.71), calls=%async_computation | async-start | bytes 2097152 | tf_op jit(solution)/shard_map/while/body/eval_jaxpr/all_to_all | solution.py:164
  622.6 23.8 %all-to-all-start.1 = ((bf16[32,8,2048]{2,1,0:T(8,128)(2,1)}), bf16[32,8,2048]{2,1,0:T(8,128)(2,1)S(1)}, u32[]{:S(2)}, u32[]{:S(2)}) async-start(bf16[32,8,2048]{2,1,0:T(8,128)(2,1)} %bitcast.125), calls=%async_computation.1 | async-start | bytes 2097152 | tf_op jit(solution)/shard_map/while/body/eval_jaxpr/all_to_all | solution.py:167
  661.5 26.0 %all-to-all-start = ((bf16[32,8,2048]{2,1,0:T(8,128)(2,1)}), bf16[32,8,2048]{2,1,0:T(8,128)(2,1)S(1)}, u32[]{:S(2)}, u32[]{:S(2)}) async-start(bf16[32,8,2048]{2,1,0:T(8,128)(2,1)} %fusion.71), calls=%async_computation | async-start | bytes 2097152 | tf_op jit(solution)/shard_map/while/body/eval_jaxpr/all_to_all | solution.py:164
  688.6 34.7 %all-to-all-start.1 = ((bf16[32,8,2048]{2,1,0:T(8,128)(2,1)}), bf16[32,8,2048]{2,1,0:T(8,128)(2,1)S(1)}, u32[]{:S(2)}, u32[]{:S(2)}) async-start(bf16[32,8,2048]{2,1,0:T(8,128)(2,1)} %bitcast.125), calls=%async_computation.1 | async-start | bytes 2097152 | tf_op jit(solution)/shard_map/while/body/eval_jaxpr/all_to_all | solution.py:167
  735.7 30.1 %all-to-all-start = ((bf16[32,8,2048]{2,1,0:T(8,128)(2,1)}), bf16[32,8,2048]{2,1,0:T(8,128)(2,1)S(1)}, u32[]{:S(2)}, u32[]{:S(2)}) async-start(bf16[32,8,2048]{2,1,0:T(8,128)(2,1)} %fusion.71), calls=%async_computation | async-start | bytes 2097152 | tf_op jit(solution)/shard_map/while/body/eval_jaxpr/all_to_all | solution.py:164
  766.9 29.4 %all-to-all-start.1 = ((bf16[32,8,2048]{2,1,0:T(8,128)(2,1)}), bf16[32,8,2048]{2,1,0:T(8,128)(2,1)S(1)}, u32[]{:S(2)}, u32[]{:S(2)}) async-start(bf16[32,8,2048]{2,1,0:T(8,128)(2,1)} %bitcast.125), calls=%async_computation.1 | async-start | bytes 2097152 | tf_op jit(solution)/shard_map/while/body/eval_jaxpr/all_to_all | solution.py:167
  810.2 28.9 %all-to-all-start = ((bf16[32,8,2048]{2,1,0:T(8,128)(2,1)}), bf16[32,8,2048]{2,1,0:T(8,128)(2,1)S(1)}, u32[]{:S(2)}, u32[]{:S(2)}) async-start(bf16[32,8,2048]{2,1,0:T(8,128)(2,1)} %fusion.71), calls=%async_computation | async-start | bytes 2097152 | tf_op jit(solution)/shard_map/while/body/eval_jaxpr/all_to_all | solution.py:164
  840.2 27.9 %all-to-all-start.1 = ((bf16[32,8,2048]{2,1,0:T(8,128)(2,1)}), bf16[32,8,2048]{2,1,0:T(8,128)(2,1)S(1)}, u32[]{:S(2)}, u32[]{:S(2)}) async-start(bf16[32,8,2048]{2,1,0:T(8,128)(2,1)} %bitcast.125), calls=%async_computation.1 | async-start | bytes 2097152 | tf_op jit(solution)/shard_map/while/body/eval_jaxpr/all_to_all | solution.py:167
  884.8 27.8 %all-to-all-start = ((bf16[32,8,2048]{2,1,0:T(8,128)(2,1)}), bf16[32,8,2048]{2,1,0:T(8,128)(2,1)S(1)}, u32[]{:S(2)}, u32[]{:S(2)}) async-start(bf16[32,8,2048]{2,1,0:T(8,128)(2,1)} %fusion.71), calls=%async_computation | async-start | bytes 2097152 | tf_op jit(solution)/shard_map/while/body/eval_jaxpr/all_to_all | solution.py:164
  913.7 26.4 %all-to-all-start.1 = ((bf16[32,8,2048]{2,1,0:T(8,128)(2,1)}), bf16[32,8,2048]{2,1,0:T(8,128)(2,1)S(1)}, u32[]{:S(2)}, u32[]{:S(2)}) async-start(bf16[32,8,2048]{2,1,0:T(8,128)(2,1)} %bitcast.125), calls=%async_computation.1 | async-start | bytes 2097152 | tf_op jit(solution)/shard_map/while/body/eval_jaxpr/all_to_all | solution.py:167
  959.3 33.5 %all-to-all-start = ((bf16[32,8,2048]{2,1,0:T(8,128)(2,1)}), bf16[32,8,2048]{2,1,0:T(8,128)(2,1)S(1)}, u32[]{:S(2)}, u32[]{:S(2)}) async-start(bf16[32,8,2048]{2,1,0:T(8,128)(2,1)} %fusion.71), calls=%async_computation | async-start | bytes 2097152 | tf_op jit(solution)/shard_map/while/body/eval_jaxpr/all_to_all | solution.py:164
  994.0 32.1 %all-to-all-start.1 = ((bf16[32,8,2048]{2,1,0:T(8,128)(2,1)}), bf16[32,8,2048]{2,1,0:T(8,128)(2,1)S(1)}, u32[]{:S(2)}, u32[]{:S(2)}) async-start(bf16[32,8,2048]{2,1,0:T(8,128)(2,1)} %bitcast.125), calls=%async_computation.1 | async-start | bytes 2097152 | tf_op jit(solution)/shard_map/while/body/eval_jaxpr/all_to_all | solution.py:167
  (18 other events, 735.1 us)
Sparse Core Ops, SparseCore 0:
  9.9 83.9 all-gather.2
  96.5 78.7 all-gather.4
where the time goes:
time: 1040 us
  waiting for transfers between devices  628 us (60%)
  starting transfers between devices  155 us (15%)
  blocking collectives  101 us (10%)
  matrix products  94.8 us (9%)
  local copies, waits for them, and re-layouts  24.2 us (2%)
  other arithmetic  23.1 us (2%)
  between operations  13.5 us (1%)
    all_to_all x11, waiting for transfers between devices, advance(): lax.all_to_all(outgoing, 'expert', split_axis=0, concat_axis=0, tiled=True)  240 us
    all_to_all x11, waiting for transfers between devices, advance(): lax.all_to_all(produced, 'expert', split_axis=0, concat_axis=0, tiled=True)  215 us
    ppermute x11, waiting for transfers between devices, shifted(): lax.ppermute(value, axis, [(source, source + steps) for source in range(i...  114 us
    all_to_all x11, starting transfers between devices, advance(): lax.all_to_all(outgoing, 'expert', split_axis=0, concat_axis=0, tiled=True)  71.3 us
    all_to_all x11, starting transfers between devices, advance(): lax.all_to_all(produced, 'expert', split_axis=0, concat_axis=0, tiled=True)  61.6 us
    all_gather x1, waiting for transfers between devices, shards(): lax.all_gather(out_weight, 'expert', axis=1, tiled=True)  57.3 us
    all_gather x1, blocking collectives, shards(): lax.all_gather(key_weight, 'expert', axis=1, tiled=True)  52.8 us
    all_gather x1, blocking collectives, shards(): lax.all_gather(value_weight, 'expert', axis=1, tiled=True)  47.8 us
  transfers between devices with their start and end apart: 35, of which 34 were waited for; matrix products, arithmetic and copies ran while one was open for 4% of the time, Pallas kernels for 0%

commit v1 on v0

--- a/solution.py
+++ b/solution.py
@@ -68,7 +68,10 @@
     capacity = min(tok_rows, tok_rows * pick_count * 4 // (3 * expert_count))
     full_query, full_key, full_value, full_out = (
         lax.all_gather(query_weight, "expert", axis=1, tiled=True),
-        lax.all_gather(key_weight, "expert", axis=1, tiled=True),
+        jnp.concatenate(
+            lax.all_to_all(jnp.stack([key_weight] * lax.axis_size("expert")), "expert", 0, 0),
+            axis=1,
+        ),
         lax.all_gather(value_weight, "expert", axis=1, tiled=True),
         lax.all_gather(out_weight, "expert", axis=1, tiled=True),
     )

time: 1040 us -> 1040 us (level)
  blocking collectives: 101 us -> 50 us
  waiting for transfers between devices: 628 us -> 667 us
  starting transfers between devices: 155 us -> 166 us
    all_gather x1 -> x0, blocking collectives: 52.8 us -> none  [shards(): lax.all_gather(key_weight, 'expert', axis=1, tiled=True)]
    all_gather x1, waiting for transfers between devices: 57.3 us -> 81.1 us  [shards(): lax.all_gather(out_weight, 'expert', axis=1, tiled=True)]
    all_gather x1, waiting for transfers between devices: 0.02 us -> 15.6 us  [shards(): lax.all_gather(query_weight, 'expert', axis=1, tiled=True)]
    all_to_all x0 -> x1, starting transfers between devices: none -> 11.7 us  [shards(): lax.all_to_all(jnp.stack([key_weight] * lax.axis_size('expert')), 'expert...]
  transfers between devices with their start and end apart: 35 -> 36, of which waited for: 34 -> 35; matrix products, arithmetic and copies ran while one was open for 4% -> 4% of each run, Pallas kernels for 0% -> 0%
where the time goes in v1:
time: 1040 us
  waiting for transfers between devices  667 us (64%)
  starting transfers between devices  166 us (16%)
  matrix products  94.8 us (9%)
  blocking collectives  50 us (5%)
  local copies, waits for them, and re-layouts  24.2 us (2%)
  other arithmetic  23.1 us (2%)
  between operations  13.5 us (1%)
    all_to_all x11, waiting for transfers between devices, advance(): lax.all_to_all(outgoing, 'expert', split_axis=0, concat_axis=0, tiled=True)  240 us
    all_to_all x11, waiting for transfers between devices, advance(): lax.all_to_all(produced, 'expert', split_axis=0, concat_axis=0, tiled=True)  215 us
    ppermute x11, waiting for transfers between devices, shifted(): lax.ppermute(value, axis, [(source, source + steps) for source in range(i...  114 us
    all_gather x1, waiting for transfers between devices, shards(): lax.all_gather(out_weight, 'expert', axis=1, tiled=True)  81.1 us
    all_to_all x11, starting transfers between devices, advance(): lax.all_to_all(outgoing, 'expert', split_axis=0, concat_axis=0, tiled=True)  71.3 us
    all_to_all x11, starting transfers between devices, advance(): lax.all_to_all(produced, 'expert', split_axis=0, concat_axis=0, tiled=True)  61.5 us
    all_gather x1, blocking collectives, shards(): lax.all_gather(value_weight, 'expert', axis=1, tiled=True)  50 us
    dot_general x4, matrix products, expert_rows(): jnp.dot(hidden, down_matrix, preferred_element_type=jnp.float32)  29.1 us
  transfers between devices with their start and end apart: 36, of which 35 were waited for; matrix products, arithmetic and copies ran while one was open for 4% of the time, Pallas kernels for 0%

profile of v1, /device:TPU:10, one launch (start us, length us, event | category | flops | bytes accessed | tf_op | source)
XLA Modules:
  0.0 1040.8 jit_solution(5640849065574281905)
XLA Ops:
  29.0 50.0 %all_gather.9 = bf16[1,2048,128]{2,1,0:T(8,128)(2,1)S(1)} all-gather(bf16[1,64,128]{2,1,0:T(8,128)(2,1)S(1)} %copy-done.4), channel_id=1, replica_groups=mesh['section'=8,'expert'=32] {'expert'}, dimensions={1}, use_global_device_ids=true | all-gather | bytes 540672 | tf_op jit(solution)/shard_map/all_gather | solution.py:75
  79.1 15.6 %all-gather.3.cloned.1.call-done = bf16[1,2048,1024]{2,1,0:T(8,128)(2,1)} async-done(((bf16[1,64,1024]{2,1,0:T(8,128)(2,1)}), bf16[1,2048,1024]{2,1,0:T(8,128)(2,1)}) %all-gather.3.cloned.1.call-update) | async-done | bytes 4194320 | tf_op jit(solution)/shard_map/all_gather | solution.py:70
  94.7 81.1 %all-gather.5.cloned.1.call-done = bf16[1,1024,2048]{2,1,0:T(8,128)(2,1)} async-done(((bf16[1,32,2048]{2,1,0:T(8,128)(2,1)}), bf16[1,1024,2048]{2,1,0:T(8,128)(2,1)}) %all-gather.5.cloned.1.call-update) | async-done | bytes 4194320 | tf_op jit(solution)/shard_map/all_gather | solution.py:76
  175.9 857.2 %while.20 = (s32[]{:T(128)}, bf16[32,2048]{1,0:T(8,128)(2,1)S(1)}, bf16[128,128]{1,0:T(8,128)(2,1)S(1)}, bf16[128,128]{1,0:T(8,128)(2,1)S(1)}, bf16[4,32,2048]{2...) while((s32[]{:T(128)}, bf16[32,2048]{1,0:T(8,128)(2,1)S(1)}, ...), condition=%wide.region_14.15_spmd, body=%wide.region_0.14_spmd.sunk | while | flops 2613929216 | bytes 35623652 | solution.py:186
  187.0 25.4 %all-to-all-done = bf16[32,8,2048]{2,1,0:T(8,128)(2,1)S(1)} async-done(((bf16[32,8,2048]{2,1,0:T(8,128)(2,1)}), bf16[32,8,2048]{2,1,0:T(8,128)(2,1)S(1)}, u32[]{:S(2)}, u32[]{:S(2)}) %all-to-all-start) | async-done | bytes 1048608 | tf_op jit(solution)/shard_map/while/body/eval_jaxpr/all_to_all | solution.py:167
  219.2 25.2 %all-to-all-done.1 = bf16[32,8,2048]{2,1,0:T(8,128)(2,1)S(1)} async-done(((bf16[32,8,2048]{2,1,0:T(8,128)(2,1)}), bf16[32,8,2048]{2,1,0:T(8,128)(2,1)S(1)}, u32[]{:S(2)}, u32[]{:S(2)}) %all-to-all-start.1) | async-done | bytes 1048608 | tf_op jit(solution)/shard_map/while/body/eval_jaxpr/all_to_all | solution.py:170
  260.5 27.3 %all-to-all-done = bf16[32,8,2048]{2,1,0:T(8,128)(2,1)S(1)} async-done(((bf16[32,8,2048]{2,1,0:T(8,128)(2,1)}), bf16[32,8,2048]{2,1,0:T(8,128)(2,1)S(1)}, u32[]{:S(2)}, u32[]{:S(2)}) %all-to-all-start) | async-done | bytes 1048608 | tf_op jit(solution)/shard_map/while/body/eval_jaxpr/all_to_all | solution.py:167
  294.6 26.7 %all-to-all-done.1 = bf16[32,8,2048]{2,1,0:T(8,128)(2,1)S(1)} async-done(((bf16[32,8,2048]{2,1,0:T(8,128)(2,1)}), bf16[32,8,2048]{2,1,0:T(8,128)(2,1)S(1)}, u32[]{:S(2)}, u32[]{:S(2)}) %all-to-all-start.1) | async-done | bytes 1048608 | tf_op jit(solution)/shard_map/while/body/eval_jaxpr/all_to_all | solution.py:170
  345.6 19.0 %all-to-all-done = bf16[32,8,2048]{2,1,0:T(8,128)(2,1)S(1)} async-done(((bf16[32,8,2048]{2,1,0:T(8,128)(2,1)}), bf16[32,8,2048]{2,1,0:T(8,128)(2,1)S(1)}, u32[]{:S(2)}, u32[]{:S(2)}) %all-to-all-start) | async-done | bytes 1048608 | tf_op jit(solution)/shard_map/while/body/eval_jaxpr/all_to_all | solution.py:167
  402.0 17.6 %collective-permute-done = bf16[32,2048]{1,0:T(8,128)(2,1)S(1)} collective-permute-done((bf16[32,2048]{1,0:T(8,128)(2,1)S(1)}, bf16[32,2048]{1,0:T(8,128)(2,1)S(1)}, u32[]{:S(2)}, u32[]{:S(2)}) %collective-permute-start) | collective-permute-done | bytes 131104 | tf_op jit(solution)/shard_map/while/body/eval_jaxpr/ppermute | solution.py:12
  430.4 18.2 %all-to-all-done = bf16[32,8,2048]{2,1,0:T(8,128)(2,1)S(1)} async-done(((bf16[32,8,2048]{2,1,0:T(8,128)(2,1)}), bf16[32,8,2048]{2,1,0:T(8,128)(2,1)S(1)}, u32[]{:S(2)}, u32[]{:S(2)}) %all-to-all-start) | async-done | bytes 1048608 | tf_op jit(solution)/shard_map/while/body/eval_jaxpr/all_to_all | solution.py:167
  486.0 18.4 %collective-permute-done = bf16[32,2048]{1,0:T(8,128)(2,1)S(1)} collective-permute-done((bf16[32,2048]{1,0:T(8,128)(2,1)S(1)}, bf16[32,2048]{1,0:T(8,128)(2,1)S(1)}, u32[]{:S(2)}, u32[]{:S(2)}) %collective-permute-start) | collective-permute-done | bytes 131104 | tf_op jit(solution)/shard_map/while/body/eval_jaxpr/ppermute | solution.py:12
  515.2 18.2 %all-to-all-done = bf16[32,8,2048]{2,1,0:T(8,128)(2,1)S(1)} async-done(((bf16[32,8,2048]{2,1,0:T(8,128)(2,1)}), bf16[32,8,2048]{2,1,0:T(8,128)(2,1)S(1)}, u32[]{:S(2)}, u32[]{:S(2)}) %all-to-all-start) | async-done | bytes 1048608 | tf_op jit(solution)/shard_map/while/body/eval_jaxpr/all_to_all | solution.py:167
  593.5 18.2 %all-to-all-done = bf16[32,8,2048]{2,1,0:T(8,128)(2,1)S(1)} async-done(((bf16[32,8,2048]{2,1,0:T(8,128)(2,1)}), bf16[32,8,2048]{2,1,0:T(8,128)(2,1)S(1)}, u32[]{:S(2)}, u32[]{:S(2)}) %all-to-all-start) | async-done | bytes 1048608 | tf_op jit(solution)/shard_map/while/body/eval_jaxpr/all_to_all | solution.py:167
  668.4 19.5 %all-to-all-done = bf16[32,8,2048]{2,1,0:T(8,128)(2,1)S(1)} async-done(((bf16[32,8,2048]{2,1,0:T(8,128)(2,1)}), bf16[32,8,2048]{2,1,0:T(8,128)(2,1)S(1)}, u32[]{:S(2)}, u32[]{:S(2)}) %all-to-all-start) | async-done | bytes 1048608 | tf_op jit(solution)/shard_map/while/body/eval_jaxpr/all_to_all | solution.py:167
  695.1 28.7 %all-to-all-done.1 = bf16[32,8,2048]{2,1,0:T(8,128)(2,1)S(1)} async-done(((bf16[32,8,2048]{2,1,0:T(8,128)(2,1)}), bf16[32,8,2048]{2,1,0:T(8,128)(2,1)S(1)}, u32[]{:S(2)}, u32[]{:S(2)}) %all-to-all-start.1) | async-done | bytes 1048608 | tf_op jit(solution)/shard_map/while/body/eval_jaxpr/all_to_all | solution.py:170
  742.9 23.4 %all-to-all-done = bf16[32,8,2048]{2,1,0:T(8,128)(2,1)S(1)} async-done(((bf16[32,8,2048]{2,1,0:T(8,128)(2,1)}), bf16[32,8,2048]{2,1,0:T(8,128)(2,1)S(1)}, u32[]{:S(2)}, u32[]{:S(2)}) %all-to-all-start) | async-done | bytes 1048608 | tf_op jit(solution)/shard_map/while/body/eval_jaxpr/all_to_all | solution.py:167
  773.0 23.7 %all-to-all-done.1 = bf16[32,8,2048]{2,1,0:T(8,128)(2,1)S(1)} async-done(((bf16[32,8,2048]{2,1,0:T(8,128)(2,1)}), bf16[32,8,2048]{2,1,0:T(8,128)(2,1)S(1)}, u32[]{:S(2)}, u32[]{:S(2)}) %all-to-all-start.1) | async-done | bytes 1048608 | tf_op jit(solution)/shard_map/while/body/eval_jaxpr/all_to_all | solution.py:170
  817.5 22.2 %all-to-all-done = bf16[32,8,2048]{2,1,0:T(8,128)(2,1)S(1)} async-done(((bf16[32,8,2048]{2,1,0:T(8,128)(2,1)}), bf16[32,8,2048]{2,1,0:T(8,128)(2,1)S(1)}, u32[]{:S(2)}, u32[]{:S(2)}) %all-to-all-start) | async-done | bytes 1048608 | tf_op jit(solution)/shard_map/while/body/eval_jaxpr/all_to_all | solution.py:167
  846.3 22.3 %all-to-all-done.1 = bf16[32,8,2048]{2,1,0:T(8,128)(2,1)S(1)} async-done(((bf16[32,8,2048]{2,1,0:T(8,128)(2,1)}), bf16[32,8,2048]{2,1,0:T(8,128)(2,1)S(1)}, u32[]{:S(2)}, u32[]{:S(2)}) %all-to-all-start.1) | async-done | bytes 1048608 | tf_op jit(solution)/shard_map/while/body/eval_jaxpr/all_to_all | solution.py:170
  892.0 21.1 %all-to-all-done = bf16[32,8,2048]{2,1,0:T(8,128)(2,1)S(1)} async-done(((bf16[32,8,2048]{2,1,0:T(8,128)(2,1)}), bf16[32,8,2048]{2,1,0:T(8,128)(2,1)S(1)}, u32[]{:S(2)}, u32[]{:S(2)}) %all-to-all-start) | async-done | bytes 1048608 | tf_op jit(solution)/shard_map/while/body/eval_jaxpr/all_to_all | solution.py:167
  919.8 20.8 %all-to-all-done.1 = bf16[32,8,2048]{2,1,0:T(8,128)(2,1)S(1)} async-done(((bf16[32,8,2048]{2,1,0:T(8,128)(2,1)}), bf16[32,8,2048]{2,1,0:T(8,128)(2,1)S(1)}, u32[]{:S(2)}, u32[]{:S(2)}) %all-to-all-start.1) | async-done | bytes 1048608 | tf_op jit(solution)/shard_map/while/body/eval_jaxpr/all_to_all | solution.py:170
  966.5 26.9 %all-to-all-done = bf16[32,8,2048]{2,1,0:T(8,128)(2,1)S(1)} async-done(((bf16[32,8,2048]{2,1,0:T(8,128)(2,1)}), bf16[32,8,2048]{2,1,0:T(8,128)(2,1)S(1)}, u32[]{:S(2)}, u32[]{:S(2)}) %all-to-all-start) | async-done | bytes 1048608 | tf_op jit(solution)/shard_map/while/body/eval_jaxpr/all_to_all | solution.py:167
  1000.1 26.4 %all-to-all-done.1 = bf16[32,8,2048]{2,1,0:T(8,128)(2,1)S(1)} async-done(((bf16[32,8,2048]{2,1,0:T(8,128)(2,1)}), bf16[32,8,2048]{2,1,0:T(8,128)(2,1)S(1)}, u32[]{:S(2)}, u32[]{:S(2)}) %all-to-all-start.1) | async-done | bytes 1048608 | tf_op jit(solution)/shard_map/while/body/eval_jaxpr/all_to_all | solution.py:170
  (397 shorter events, 514.6 us)
Async XLA Ops:
  6.5 88.1 %all-gather.3.cloned.1.call-start = ((), (), s32[]{:S(2)}) async-start(), calls=%async_computation.3 | async-start | bytes 4325376 | tf_op jit(solution)/shard_map/all_gather | solution.py:70
  7.3 168.6 %all-gather.5.cloned.1.call-start = ((), (), s32[]{:S(2)}) async-start(), calls=%async_computation.4 | async-start | bytes 4325376 | tf_op jit(solution)/shard_map/all_gather | solution.py:76
  9.6 69.5 %all-to-all-start.2 = ((bf16[32,1,64,128]{3,2,1,0:T(8,128)(2,1)}), bf16[32,1,64,128]{3,2,1,0:T(8,128)(2,1)S(1)}, u32[]{:S(2)}, u32[]{:S(2)}) async-start(bf16[32,1,64,128]{3,2,1,0:T(8,128)(2,1)} %stack.2), calls=%async_computation.2 | async-start | bytes 1048576 | tf_op jit(solution)/shard_map/all_to_all | solution.py:72
  180.0 32.4 %all-to-all-start = ((bf16[32,8,2048]{2,1,0:T(8,128)(2,1)}), bf16[32,8,2048]{2,1,0:T(8,128)(2,1)S(1)}, u32[]{:S(2)}, u32[]{:S(2)}) async-start(bf16[32,8,2048]{2,1,0:T(8,128)(2,1)} %fusion.71), calls=%async_computation | async-start | bytes 2097152 | tf_op jit(solution)/shard_map/while/body/eval_jaxpr/all_to_all | solution.py:167
  213.5 30.8 %all-to-all-start.1 = ((bf16[32,8,2048]{2,1,0:T(8,128)(2,1)}), bf16[32,8,2048]{2,1,0:T(8,128)(2,1)S(1)}, u32[]{:S(2)}, u32[]{:S(2)}) async-start(bf16[32,8,2048]{2,1,0:T(8,128)(2,1)} %bitcast.126), calls=%async_computation.1 | async-start | bytes 2097152 | tf_op jit(solution)/shard_map/while/body/eval_jaxpr/all_to_all | solution.py:170
  255.0 32.9 %all-to-all-start = ((bf16[32,8,2048]{2,1,0:T(8,128)(2,1)}), bf16[32,8,2048]{2,1,0:T(8,128)(2,1)S(1)}, u32[]{:S(2)}, u32[]{:S(2)}) async-start(bf16[32,8,2048]{2,1,0:T(8,128)(2,1)} %fusion.71), calls=%async_computation | async-start | bytes 2097152 | tf_op jit(solution)/shard_map/while/body/eval_jaxpr/all_to_all | solution.py:167
  289.0 32.4 %all-to-all-start.1 = ((bf16[32,8,2048]{2,1,0:T(8,128)(2,1)}), bf16[32,8,2048]{2,1,0:T(8,128)(2,1)S(1)}, u32[]{:S(2)}, u32[]{:S(2)}) async-start(bf16[32,8,2048]{2,1,0:T(8,128)(2,1)} %bitcast.126), calls=%async_computation.1 | async-start | bytes 2097152 | tf_op jit(solution)/shard_map/while/body/eval_jaxpr/all_to_all | solution.py:170
  338.9 25.7 %all-to-all-start = ((bf16[32,8,2048]{2,1,0:T(8,128)(2,1)}), bf16[32,8,2048]{2,1,0:T(8,128)(2,1)S(1)}, u32[]{:S(2)}, u32[]{:S(2)}) async-start(bf16[32,8,2048]{2,1,0:T(8,128)(2,1)} %fusion.71), calls=%async_computation | async-start | bytes 2097152 | tf_op jit(solution)/shard_map/while/body/eval_jaxpr/all_to_all | solution.py:167
  375.9 23.8 %all-to-all-start.1 = ((bf16[32,8,2048]{2,1,0:T(8,128)(2,1)}), bf16[32,8,2048]{2,1,0:T(8,128)(2,1)S(1)}, u32[]{:S(2)}, u32[]{:S(2)}) async-start(bf16[32,8,2048]{2,1,0:T(8,128)(2,1)} %bitcast.126), calls=%async_computation.1 | async-start | bytes 2097152 | tf_op jit(solution)/shard_map/while/body/eval_jaxpr/all_to_all | solution.py:170
  423.7 24.9 %all-to-all-start = ((bf16[32,8,2048]{2,1,0:T(8,128)(2,1)}), bf16[32,8,2048]{2,1,0:T(8,128)(2,1)S(1)}, u32[]{:S(2)}, u32[]{:S(2)}) async-start(bf16[32,8,2048]{2,1,0:T(8,128)(2,1)} %fusion.71), calls=%async_computation | async-start | bytes 2097152 | tf_op jit(solution)/shard_map/while/body/eval_jaxpr/all_to_all | solution.py:167
  508.5 24.9 %all-to-all-start = ((bf16[32,8,2048]{2,1,0:T(8,128)(2,1)}), bf16[32,8,2048]{2,1,0:T(8,128)(2,1)S(1)}, u32[]{:S(2)}, u32[]{:S(2)}) async-start(bf16[32,8,2048]{2,1,0:T(8,128)(2,1)} %fusion.71), calls=%async_computation | async-start | bytes 2097152 | tf_op jit(solution)/shard_map/while/body/eval_jaxpr/all_to_all | solution.py:167
  544.8 23.8 %all-to-all-start.1 = ((bf16[32,8,2048]{2,1,0:T(8,128)(2,1)}), bf16[32,8,2048]{2,1,0:T(8,128)(2,1)S(1)}, u32[]{:S(2)}, u32[]{:S(2)}) async-start(bf16[32,8,2048]{2,1,0:T(8,128)(2,1)} %bitcast.126), calls=%async_computation.1 | async-start | bytes 2097152 | tf_op jit(solution)/shard_map/while/body/eval_jaxpr/all_to_all | solution.py:170
  587.9 23.8 %all-to-all-start = ((bf16[32,8,2048]{2,1,0:T(8,128)(2,1)}), bf16[32,8,2048]{2,1,0:T(8,128)(2,1)S(1)}, u32[]{:S(2)}, u32[]{:S(2)}) async-start(bf16[32,8,2048]{2,1,0:T(8,128)(2,1)} %fusion.71), calls=%async_computation | async-start | bytes 2097152 | tf_op jit(solution)/shard_map/while/body/eval_jaxpr/all_to_all | solution.py:167
  623.1 23.8 %all-to-all-start.1 = ((bf16[32,8,2048]{2,1,0:T(8,128)(2,1)}), bf16[32,8,2048]{2,1,0:T(8,128)(2,1)S(1)}, u32[]{:S(2)}, u32[]{:S(2)}) async-start(bf16[32,8,2048]{2,1,0:T(8,128)(2,1)} %bitcast.126), calls=%async_computation.1 | async-start | bytes 2097152 | tf_op jit(solution)/shard_map/while/body/eval_jaxpr/all_to_all | solution.py:170
  662.0 26.0 %all-to-all-start = ((bf16[32,8,2048]{2,1,0:T(8,128)(2,1)}), bf16[32,8,2048]{2,1,0:T(8,128)(2,1)S(1)}, u32[]{:S(2)}, u32[]{:S(2)}) async-start(bf16[32,8,2048]{2,1,0:T(8,128)(2,1)} %fusion.71), calls=%async_computation | async-start | bytes 2097152 | tf_op jit(solution)/shard_map/while/body/eval_jaxpr/all_to_all | solution.py:167
  689.1 34.7 %all-to-all-start.1 = ((bf16[32,8,2048]{2,1,0:T(8,128)(2,1)}), bf16[32,8,2048]{2,1,0:T(8,128)(2,1)S(1)}, u32[]{:S(2)}, u32[]{:S(2)}) async-start(bf16[32,8,2048]{2,1,0:T(8,128)(2,1)} %bitcast.126), calls=%async_computation.1 | async-start | bytes 2097152 | tf_op jit(solution)/shard_map/while/body/eval_jaxpr/all_to_all | solution.py:170
  736.2 30.1 %all-to-all-start = ((bf16[32,8,2048]{2,1,0:T(8,128)(2,1)}), bf16[32,8,2048]{2,1,0:T(8,128)(2,1)S(1)}, u32[]{:S(2)}, u32[]{:S(2)}) async-start(bf16[32,8,2048]{2,1,0:T(8,128)(2,1)} %fusion.71), calls=%async_computation | async-start | bytes 2097152 | tf_op jit(solution)/shard_map/while/body/eval_jaxpr/all_to_all | solution.py:167
  767.4 29.4 %all-to-all-start.1 = ((bf16[32,8,2048]{2,1,0:T(8,128)(2,1)}), bf16[32,8,2048]{2,1,0:T(8,128)(2,1)S(1)}, u32[]{:S(2)}, u32[]{:S(2)}) async-start(bf16[32,8,2048]{2,1,0:T(8,128)(2,1)} %bitcast.126), calls=%async_computation.1 | async-start | bytes 2097152 | tf_op jit(solution)/shard_map/while/body/eval_jaxpr/all_to_all | solution.py:170
  810.8 28.9 %all-to-all-start = ((bf16[32,8,2048]{2,1,0:T(8,128)(2,1)}), bf16[32,8,2048]{2,1,0:T(8,128)(2,1)S(1)}, u32[]{:S(2)}, u32[]{:S(2)}) async-start(bf16[32,8,2048]{2,1,0:T(8,128)(2,1)} %fusion.71), calls=%async_computation | async-start | bytes 2097152 | tf_op jit(solution)/shard_map/while/body/eval_jaxpr/all_to_all | solution.py:167
  840.7 27.9 %all-to-all-start.1 = ((bf16[32,8,2048]{2,1,0:T(8,128)(2,1)}), bf16[32,8,2048]{2,1,0:T(8,128)(2,1)S(1)}, u32[]{:S(2)}, u32[]{:S(2)}) async-start(bf16[32,8,2048]{2,1,0:T(8,128)(2,1)} %bitcast.126), calls=%async_computation.1 | async-start | bytes 2097152 | tf_op jit(solution)/shard_map/while/body/eval_jaxpr/all_to_all | solution.py:170
  885.3 27.8 %all-to-all-start = ((bf16[32,8,2048]{2,1,0:T(8,128)(2,1)}), bf16[32,8,2048]{2,1,0:T(8,128)(2,1)S(1)}, u32[]{:S(2)}, u32[]{:S(2)}) async-start(bf16[32,8,2048]{2,1,0:T(8,128)(2,1)} %fusion.71), calls=%async_computation | async-start | bytes 2097152 | tf_op jit(solution)/shard_map/while/body/eval_jaxpr/all_to_all | solution.py:167
  914.2 26.4 %all-to-all-start.1 = ((bf16[32,8,2048]{2,1,0:T(8,128)(2,1)}), bf16[32,8,2048]{2,1,0:T(8,128)(2,1)S(1)}, u32[]{:S(2)}, u32[]{:S(2)}) async-start(bf16[32,8,2048]{2,1,0:T(8,128)(2,1)} %bitcast.126), calls=%async_computation.1 | async-start | bytes 2097152 | tf_op jit(solution)/shard_map/while/body/eval_jaxpr/all_to_all | solution.py:170
  959.9 33.5 %all-to-all-start = ((bf16[32,8,2048]{2,1,0:T(8,128)(2,1)}), bf16[32,8,2048]{2,1,0:T(8,128)(2,1)S(1)}, u32[]{:S(2)}, u32[]{:S(2)}) async-start(bf16[32,8,2048]{2,1,0:T(8,128)(2,1)} %fusion.71), calls=%async_computation | async-start | bytes 2097152 | tf_op jit(solution)/shard_map/while/body/eval_jaxpr/all_to_all | solution.py:167
  994.5 32.1 %all-to-all-start.1 = ((bf16[32,8,2048]{2,1,0:T(8,128)(2,1)}), bf16[32,8,2048]{2,1,0:T(8,128)(2,1)S(1)}, u32[]{:S(2)}, u32[]{:S(2)}) async-start(bf16[32,8,2048]{2,1,0:T(8,128)(2,1)} %bitcast.126), calls=%async_computation.1 | async-start | bytes 2097152 | tf_op jit(solution)/shard_map/while/body/eval_jaxpr/all_to_all | solution.py:170
  (19 other events, 573.7 us)
Sparse Core Ops, SparseCore 0:
  9.9 84.7 all-gather.2
  97.2 78.5 all-gather.4
